TPU v7x, 512 devices: a whole 4x4x16 slice. The times are simulated.
512 devices in a mesh: expert: 8 (over y, core), dp: 16 (over z), tensor: 4 (over x).
Axes of the slice: x: 4, y: 4, z: 16, core: 2. Of those that a mesh axis runs over, the one named last changes fastest.
Arguments:
- tokens: bfloat16 [2048, 4096], P(('expert', 'dp')), may hold values from -6 to 6
- expert_ids: int32 [2048, 2], P(('expert', 'dp')), may hold values from 0 to 7, all different within a row; in each aligned block of 16 rows (0 to 15, 16 to 31, ...) at most 6 rows name the same one
- route_weight: float32 [2048, 2], P(('expert', 'dp')), may hold values from 0.2 to 1
- gate_weight: bfloat16 [8, 4096, 8192], P('expert', None, ('dp', 'tensor')), may hold values from -0.09375 to 0.09375
- up_weight: bfloat16 [8, 4096, 8192], P('expert', None, ('dp', 'tensor')), may hold values from -0.09375 to 0.09375
- down_weight: bfloat16 [8, 8192, 4096], P('expert', 'dp', 'tensor'), may hold values from -0.125 to 0.125
- past_layers: bfloat16 [8, 2048, 4096], P(None, ('expert', 'dp'), 'tensor'), may hold values from -6 to 6
- dwa_weight: float32 [9], replicated, may hold values from 0.3 to 1.2
Outputs:
- mixed: bfloat16 [2048, 4096], P(('expert', 'dp'), 'tensor')
Inputs may be any that keep to these rules, and one draw needn't show every extreme that they name: `expert_ids`: each row names 2 different experts. In each aligned block of 16 rows (the rows of one device) no expert is named more than 6 times; in some blocks one expert is named exactly 6 times.
All inputs are finite; a program needn't handle non-finite values.
Results may differ from a plain program's by a relative error of at most 0.009.
Values may be sent and summed in bfloat16 or wider, within the bound.
No kernel may reach another device: no remote copies, remote signals or barrier semaphores. Data moves between devices by JAX's collectives and lax.ppermute only.
A program may use at most 64 MiB of HBM per device.

v0:
```python
import jax
import jax.numpy as jnp
from jax import lax
from jax.sharding import PartitionSpec as P


def from_everyone(shard, axis):
    count = lax.axis_size(axis)
    return lax.all_to_all(
        jnp.broadcast_to(shard[None], (count, *shard.shape)), axis, 0, 0, tiled=True
    )


def joined_along(tiles, dim):
    dims = list(tiles.shape[1:])
    dims[dim] *= tiles.shape[0]
    return jnp.moveaxis(tiles, 0, dim).reshape(dims)


def gathered_copies(shard, axis, dim):
    tiles = from_everyone(shard, axis)
    return joined_along(tiles, dim)


def assignment_slots(expert_ids, experts, capacity):
    flat_ids = expert_ids.reshape(-1)
    matches = (flat_ids[:, None] == jnp.arange(experts, dtype=jnp.int32)[None, :]).astype(jnp.int32)
    earlier = jnp.cumsum(matches, axis=0) - matches
    slot_ids = jnp.sum(earlier * matches, axis=1)
    return flat_ids * capacity + slot_ids


def selector(expert_ids, experts, capacity):
    targets = assignment_slots(expert_ids, experts, capacity)
    matched = targets[None, :] == jnp.arange(experts * capacity, dtype=jnp.int32)[:, None]
    chosen = matched.reshape(experts * capacity, expert_ids.shape[0], expert_ids.shape[1])
    return jnp.sum(chosen.astype(jnp.float32), axis=2).astype(jnp.bfloat16)


def per_device(
    tokens, expert_ids, route_weight, gate_weight, up_weight, down_weight, past_layers, dwa_weight
):
    experts = lax.axis_size("expert")
    tok_rows, feature_width = tokens.shape
    chosen_count = expert_ids.shape[1]
    capacity = min(tok_rows, 3 * chosen_count * tok_rows // (2 * experts))
    w_gate = gate_weight[0]
    w_up = up_weight[0]
    w_down = down_weight[0]
    targets = assignment_slots(expert_ids, experts, capacity)
    selected = selector(expert_ids, experts, capacity)
    packed = jnp.dot(selected, tokens, preferred_element_type=jnp.float32).astype(jnp.bfloat16)
    packed = packed.reshape(experts, capacity, feature_width)
    arrived = lax.all_to_all(packed, "expert", split_axis=0, concat_axis=0, tiled=True)
    block_rows = lax.all_gather(
        arrived.reshape(experts * capacity, feature_width), "dp", axis=0, tiled=True
    )
    gate = jnp.dot(block_rows, w_gate, preferred_element_type=jnp.float32)
    up = jnp.dot(block_rows, w_up, preferred_element_type=jnp.float32)
    hidden = (jax.nn.silu(gate) * up).astype(jnp.bfloat16)
    hidden_wide = gathered_copies(hidden, "tensor", 1)
    expert_out = lax.psum_scatter(
        jnp.dot(hidden_wide, w_down, preferred_element_type=jnp.float32),
        "dp",
        scatter_dimension=0,
        tiled=True,
    ).astype(jnp.bfloat16)
    quarter = expert_out.shape[1]
    returned_rows = lax.all_to_all(
        expert_out.reshape(experts, capacity, quarter),
        "expert",
        split_axis=0,
        concat_axis=0,
        tiled=True,
    )
    returned_rows = returned_rows.reshape(experts * capacity, quarter)
    fetched = returned_rows[targets].astype(jnp.float32).reshape(tok_rows, chosen_count, quarter)
    shares = route_weight / jnp.sum(route_weight, axis=1, keepdims=True)
    expert_mix = jnp.sum(fetched * shares[:, :, None], axis=1)
    first_column = lax.axis_index("tensor") * quarter
    residual = lax.dynamic_slice_in_dim(tokens, first_column, quarter, 1).astype(jnp.float32)
    current = residual + expert_mix
    depth = past_layers.shape[0]
    history = jnp.einsum("j,jtd->td", dwa_weight[:depth], past_layers.astype(jnp.float32))
    return (dwa_weight[depth] * current + history).astype(jnp.bfloat16)


def solution(mesh):
    return jax.shard_map(
        per_device,
        mesh=mesh,
        in_specs=(
            P(("expert", "dp"), None),
            P(("expert", "dp"), None),
            P(("expert", "dp"), None),
            P("expert", None, ("dp", "tensor")),
            P("expert", None, ("dp", "tensor")),
            P("expert", "dp", "tensor"),
            P(None, ("expert", "dp"), "tensor"),
            P(),
        ),
        out_specs=P(("expert", "dp"), "tensor"),
        check_vma=False,
    )
```

profile of v0, /device:TPU:1, one launch (start us, length us, event | category | flops | bytes accessed | tf_op | source)
XLA Modules:
  0.0 233.8 jit_solution(14384665700464559694)
XLA Ops:
  6.5 0.9 copy.16
  7.4 0.1 eq.15
  7.7 0.2 select_reduce_fusion
  8.1 1.2 convolution_convert_fusion
  9.3 0.1 reshape.70
  9.5 18.6 %all_to_all.15 = bf16[8,6,4096]{2,1,0:T(8,128)(2,1)S(1)} all-to-all(bf16[8,6,4096]{2,1,0:T(8,128)(2,1)S(1)} %reshape.70), channel_id=1, replica_groups=mesh['expert'=8,'dp'=16,'tensor'=4] {'expert'}, dimensions={0} | all-to-all | bytes 786432 | tf_op jit(solution)/shard_map/all_to_all | solution.py:54
  28.0 0.9 reshape.71
  29.0 82.5 %all-gather.2.cloned.1.call-done = bf16[768,4096]{1,0:T(8,128)(2,1)} async-done(((bf16[48,4096]{1,0:T(8,128)(2,1)}), bf16[768,4096]{1,0:T(8,128)(2,1)}) %all-gather.2.cloned.1.call-update) | async-done | bytes 6291472 | tf_op jit(solution)/shard_map/all_gather | solution.py:55
  111.5 5.0 %fusion.4 = f32[768,128]{1,0:T(8,128)S(1)} fusion(bf16[768,4096]{1,0:T(8,128)(2,1)} %all-gather.2.cloned.1.call-done, bf16[1,4096,128]{2,1,0:T(8,128)(2,1)} %param.11), kind=kOutput, calls=%fused_computation.7 | convolution fusion | flops 805306368 | bytes 7733248 | tf_op jit(solution)/shard_map/dot_general | solution.py:58
  116.5 1.8 fusion
  118.3 0.1 copy.19
  118.5 12.1 %all_to_all.16 = bf16[4,768,128]{1,2,0:T(8,128)(2,1)S(1)} all-to-all(bf16[4,768,128]{1,2,0:T(8,128)(2,1)S(1)} %broadcast_in_dim.2), channel_id=1, replica_groups=mesh['expert'=8,'dp'=16,'tensor'=4] {'tensor'}, dimensions={0} | all-to-all | bytes 1572864 | tf_op jit(solution)/shard_map/all_to_all | solution.py:9
  130.7 2.7 %fusion.1 = f32[768,1024]{1,0:T(8,128)} fusion(bf16[768,512]{0,1:T(8,128)(2,1)S(1)} %bitcast.31, bf16[1,512,1024]{2,1,0:T(8,128)(2,1)S(1)} %copy-done), kind=kOutput, calls=%fused_computation.4 | convolution fusion | flops 805306368 | bytes 4980736 | tf_op jit(solution)/shard_map/dot_general | solution.py:63
  133.6 0.7 slice.6
  134.2 0.3 fusion.6
  134.5 68.1 %reduce-scatter.2.cloned.1.call-done = f32[48,1024]{1,0:T(8,128)} async-done(((f32[768,1024]{1,0:T(8,128)}), f32[48,1024]{1,0:T(8,128)}) %reduce-scatter.2.cloned.1.call-update) | async-done | bytes 196624 | tf_op jit(solution)/shard_map/reduce_scatter | solution.py:62
  202.6 0.9 convert_element_type.39
  203.5 0.7 reshape.73
  204.2 14.5 %all-to-all-start.2 = ((bf16[8,6,1024]{2,1,0:T(8,128)(2,1)}), bf16[8,6,1024]{2,1,0:T(8,128)(2,1)S(1)}, u32[]{:S(2)}, u32[]{:S(2)}) async-start(bf16[8,6,1024]{2,1,0:T(8,128)(2,1)} %reshape.73), calls=%async_computation.3 | async-start | bytes 262144 | tf_op jit(solution)/shard_map/all_to_all | solution.py:69
  218.7 5.2 %all-to-all-done.2 = bf16[8,6,1024]{2,1,0:T(8,128)(2,1)S(1)} async-done(((bf16[8,6,1024]{2,1,0:T(8,128)(2,1)}), bf16[8,6,1024]{2,1,0:T(8,128)(2,1)S(1)}, u32[]{:S(2)}, u32[]{:S(2)}) %all-to-all-start.2) | async-done | bytes 98336 | tf_op jit(solution)/shard_map/all_to_all | solution.py:69
  224.0 0.6 gather_fusion
  224.6 0.1 reshape.75
  224.7 0.2 multiply_reduce_fusion
  224.9 2.0 fusion.8
  (30 shorter events, 0.8 us)
Async XLA Ops:
  6.5 124.1 %copy-start = (bf16[1,512,1024]{2,1,0:T(8,128)(2,1)S(1)}, bf16[1,512,1024]{2,1,0:T(8,128)(2,1)}, u32[]{:S(2)}) copy-start(bf16[1,512,1024]{2,1,0:T(8,128)(2,1)} %param.13) | copy-start | bytes 3145732
  6.5 109.9 %copy-start.5 = (bf16[1,4096,128]{2,1,0:T(8,128)(2,1)S(1)}, bf16[1,4096,128]{2,1,0:T(8,128)(2,1)}, u32[]{:S(2)}) copy-start(bf16[1,4096,128]{2,1,0:T(8,128)(2,1)} %param.12) | copy-start | bytes 3145732
  6.5 104.9 %all-gather.2.cloned.1.call-start = ((), (), s32[]{:S(2)}) async-start(), calls=%async_computation.4 | async-start | bytes 6684672 | tf_op jit(solution)/shard_map/all_gather | solution.py:55
  28.9 173.6 %reduce-scatter.2.cloned.1.call-start = ((), (), s32[]{:S(2)}) async-start(), calls=%async_computation.5 | async-start | bytes 3342336 | tf_op jit(solution)/shard_map/reduce_scatter | solution.py:62
  111.5 5.0 %copy-start.4 = (bf16[768,4096]{1,0:T(8,128)(2,1)S(1)}, bf16[768,4096]{1,0:T(8,128)(2,1)}, u32[]{:S(2)}) copy-start(bf16[768,4096]{1,0:T(8,128)(2,1)} %all-gather.2.cloned.1.call-done) | copy-start | bytes 18874372
  118.3 15.2 %copy-start.2 = (f32[16,2]{0,1:T(2,128)S(1)}, f32[16,2]{0,1:T(2,128)}, u32[]{:S(2)}) copy-start(f32[16,2]{0,1:T(2,128)} %param.10) | copy-start | bytes 388
  118.3 15.3 %copy-start.3 = (f32[9]{0:T(128)S(1)}, f32[9]{0:T(128)}, u32[]{:S(2)}) copy-start(f32[9]{0:T(128)} %param.15) | copy-start | bytes 112
  118.3 16.0 %copy-start.1 = (bf16[8,16,1024]{2,1,0:T(8,128)(2,1)S(1)}, bf16[8,16,1024]{2,1,0:T(8,128)(2,1)}, u32[]{:S(2)}) copy-start(bf16[8,16,1024]{2,1,0:T(8,128)(2,1)} %param.14) | copy-start | bytes 786436
  204.2 19.7 %all-to-all-start.2 = ((bf16[8,6,1024]{2,1,0:T(8,128)(2,1)}), bf16[8,6,1024]{2,1,0:T(8,128)(2,1)S(1)}, u32[]{:S(2)}, u32[]{:S(2)}) async-start(bf16[8,6,1024]{2,1,0:T(8,128)(2,1)} %reshape.73), calls=%async_computation.3 | async-start | bytes 262144 | tf_op jit(solution)/shard_map/all_to_all | solution.py:69
Sparse Core Ops, SparseCore 0:
  29.1 82.3 all-gather.1
  133.5 69.0 reduce-scatter.1
where the time goes:
time: 234 us
  waiting for transfers between devices  156 us (67%)
  blocking collectives  30.7 us (13%)
  starting transfers between devices  14.5 us (6%)
  between operations  13.5 us (6%)
  matrix products  10.9 us (5%)
  local copies, waits for them, and re-layouts  4.67 us (2%)
  other arithmetic  3.63 us (2%)
    all_gather x1, waiting for transfers between devices, per_device(): lax.all_gather(arrived.reshape(experts * capacity, feature_width), 'dp',...  82.5 us
    reduce_scatter x1, waiting for transfers between devices, per_device(): lax.psum_scatter(jnp.dot(hidden_wide, w_down, preferred_element_type=jnp....  68.1 us
    all_to_all x1, blocking collectives, per_device(): lax.all_to_all(packed, 'expert', split_axis=0, concat_axis=0, tiled=True)  18.6 us
    all_to_all x1, starting transfers between devices, per_device(): lax.all_to_all(expert_out.reshape(experts, capacity, quarter), 'expert',...  14.5 us
    all_to_all x1, blocking collectives, from_everyone(): lax.all_to_all(jnp.broadcast_to(shard[None], (count, *shard.shape)), axis...  12.1 us
    all_to_all x1, waiting for transfers between devices, per_device(): lax.all_to_all(expert_out.reshape(experts, capacity, quarter), 'expert',...  5.23 us
    dot_general x1, matrix products, per_device(): gate = jnp.dot(block_rows, w_gate, preferred_element_type=jnp.float32)  4.98 us
  transfers between devices with their start and end apart: 3, of which 3 were waited for; matrix products, arithmetic and copies ran while one was open for 0% of the time, Pallas kernels for 0%

commit v1 on v0

--- a/solution.py
+++ b/solution.py
@@ -2,6 +2,12 @@
 import jax.numpy as jnp
 from jax import lax
 from jax.sharding import PartitionSpec as P
+
+
+def joined_along_2(blocks, dim):
+    shape = list(blocks.shape[1:])
+    shape[dim] *= blocks.shape[0]
+    return jnp.moveaxis(blocks, 0, dim).reshape(shape)
 
 
 def from_everyone(shard, axis):
@@ -52,9 +58,20 @@
     packed = jnp.dot(selected, tokens, preferred_element_type=jnp.float32).astype(jnp.bfloat16)
     packed = packed.reshape(experts, capacity, feature_width)
     arrived = lax.all_to_all(packed, "expert", split_axis=0, concat_axis=0, tiled=True)
-    block_rows = lax.all_gather(
-        arrived.reshape(experts * capacity, feature_width), "dp", axis=0, tiled=True
-    )
+    shard_2 = arrived.reshape(experts * capacity, feature_width)
+    size = lax.axis_size("dp")
+    pairs = [(i, (i + 1) % size) for i in range(size)]
+    back = [(b, a) for a, b in pairs]
+    lower, upper = ([], [])
+    for step in range(size - 1):
+        if step % 2 == 0:
+            lower.append(lax.ppermute(lower[-1] if lower else shard_2, "dp", pairs))
+        else:
+            upper.append(lax.ppermute(upper[-1] if upper else shard_2, "dp", back))
+    blocks = jnp.stack([*lower[::-1], shard_2, *upper])
+    shift = lax.axis_index("dp") - len(lower)
+    blocks = blocks[(jnp.arange(size) - shift) % size]
+    block_rows = joined_along_2(blocks, 0)
     gate = jnp.dot(block_rows, w_gate, preferred_element_type=jnp.float32)
     up = jnp.dot(block_rows, w_up, preferred_element_type=jnp.float32)
     hidden = (jax.nn.silu(gate) * up).astype(jnp.bfloat16)

time: 234 us -> 271 us (1.16)
  starting transfers between devices: 14.5 us -> 62.4 us
  waiting for transfers between devices: 156 us -> 117 us
  local copies, waits for them, and re-layouts: 4.67 us -> 31.8 us
    all_gather x1 -> x0, waiting for transfers between devices: 82.5 us -> none  [per_device(): lax.all_gather(arrived.reshape(experts * capacity, feature_width), 'dp',...]
    ppermute x0 -> x15, starting transfers between devices: none -> 48.3 us  [the longest x7 33 us: per_device(): upper.append(lax.ppermute(upper[-1] if upper else shard_2, 'dp', back))]
    ppermute x0 -> x15, waiting for transfers between devices: none -> 41.2 us  [the longest x8 40.5 us: per_device(): lower.append(lax.ppermute(lower[-1] if lower else shard_2, 'dp', pairs))]
    unnamed x13 -> x46, local copies, waits for them, and re-layouts: 0.93 us -> 21.4 us
    gather x0 -> x1, local copies, waits for them, and re-layouts: none -> 6.44 us  [per_device(): blocks = blocks[(jnp.arange(size) - shift) % size]]
  transfers between devices with their start and end apart: 3 -> 17, of which waited for: 3 -> 12; matrix products, arithmetic and copies ran while one was open for 0% -> 8% of each run, Pallas kernels for 0% -> 0%
where the time goes in v1:
time: 271 us; the launch traced here: 270 us
  waiting for transfers between devices  117 us (43%)
  starting transfers between devices  62.4 us (23%)
  local copies, waits for them, and re-layouts  31.8 us (12%)
  blocking collectives  30.7 us (11%)
  between operations  13.8 us (5%)
  matrix products  10.6 us (4%)
  other arithmetic  3.71 us (1%)
    reduce_scatter x1, waiting for transfers between devices, per_device(): lax.psum_scatter(jnp.dot(hidden_wide, w_down, preferred_element_type=jnp....  70.3 us
    ppermute x8, waiting for transfers between devices, per_device(): lower.append(lax.ppermute(lower[-1] if lower else shard_2, 'dp', pairs))  40.5 us
    ppermute x7, starting transfers between devices, per_device(): upper.append(lax.ppermute(upper[-1] if upper else shard_2, 'dp', back))  33 us
    unnamed x46, local copies, waits for them, and re-layouts  21.4 us
    all_to_all x1, blocking collectives, per_device(): lax.all_to_all(packed, 'expert', split_axis=0, concat_axis=0, tiled=True)  18.6 us
    ppermute x8, starting transfers between devices, per_device(): lower.append(lax.ppermute(lower[-1] if lower else shard_2, 'dp', pairs))  15.3 us
    all_to_all x1, starting transfers between devices, per_device(): lax.all_to_all(expert_out.reshape(experts, capacity, quarter), 'expert',...  14.1 us
    all_to_all x1, blocking collectives, from_everyone(): lax.all_to_all(jnp.broadcast_to(shard[None], (count, *shard.shape)), axis...  12.2 us
  transfers between devices with their start and end apart: 17, of which 12 were waited for; matrix products, arithmetic and copies ran while one was open for 8% of the time, Pallas kernels for 0%

profile of v1, /device:TPU:1, one launch (start us, length us, event | category | flops | bytes accessed | tf_op | source)
XLA Modules:
  0.0 269.8 jit_solution(8422087766499826098)
XLA Ops:
  9.4 18.6 %all_to_all.15 = bf16[8,6,4096]{2,1,0:T(8,128)(2,1)S(1)} all-to-all(bf16[8,6,4096]{2,1,0:T(8,128)(2,1)S(1)} %reshape.122), channel_id=1, replica_groups=mesh['expert'=8,'dp'=16,'tensor'=4] {'expert'}, dimensions={0} | all-to-all | bytes 786432 | tf_op jit(solution)/shard_map/all_to_all | solution.py:60
  30.0 14.1 %collective-permute-done = bf16[48,4096]{1,0:T(8,128)(2,1)S(1)} collective-permute-done((bf16[48,4096]{1,0:T(8,128)(2,1)S(1)}, bf16[48,4096]{1,0:T(8,128)(2,1)S(1)}, u32[]{:S(2)}, u32[]{:S(2)}) %collective-permute-start) | collective-permute-done | bytes 393248 | tf_op jit(solution)/shard_map/ppermute | solution.py:68
  46.1 4.6 %collective-permute-start.8 = (bf16[48,4096]{1,0:T(8,128)(2,1)S(1)}, bf16[48,4096]{1,0:T(8,128)(2,1)S(1)}, u32[]{:S(2)}, u32[]{:S(2)}) collective-permute-start(bf16[48,4096]{1,0:T(8,128)(2,1)S(1)} %reshape.123), channel_id=1, source_target_pairs={{4,0},{8,4},{12,8},{16,12},{20,16},{24,20},{28,24},{32,28},{36,32}... | collective-permute-start | bytes 1179656 | tf_op jit(solution)/shard_map/ppermute | solution.py:70
  50.7 5.7 %collective-permute-done.1 = bf16[48,4096]{1,0:T(8,128)(2,1)S(1)} collective-permute-done((bf16[48,4096]{1,0:T(8,128)(2,1)S(1)}, bf16[48,4096]{1,0:T(8,128)(2,1)S(1)}, u32[]{:S(2)}, u32[]{:S(2)}) %collective-permute-start.1) | collective-permute-done | bytes 393248 | tf_op jit(solution)/shard_map/ppermute | solution.py:68
  58.3 4.6 %collective-permute-start.9 = (bf16[48,4096]{1,0:T(8,128)(2,1)S(1)}, bf16[48,4096]{1,0:T(8,128)(2,1)S(1)}, u32[]{:S(2)}, u32[]{:S(2)}) collective-permute-start(bf16[48,4096]{1,0:T(8,128)(2,1)S(1)} %collective-permute-done.8), channel_id=1, source_target_pairs={{4,0},{8,4},{12,8},{16,12},{20,16},{24,20},{28,24},{32,28},{36,32}... | collective-permute-start | bytes 1179656 | tf_op jit(solution)/shard_map/ppermute | solution.py:70
  62.8 4.8 %collective-permute-done.2 = bf16[48,4096]{1,0:T(8,128)(2,1)S(1)} collective-permute-done((bf16[48,4096]{1,0:T(8,128)(2,1)S(1)}, bf16[48,4096]{1,0:T(8,128)(2,1)S(1)}, u32[]{:S(2)}, u32[]{:S(2)}) %collective-permute-start.2) | collective-permute-done | bytes 393248 | tf_op jit(solution)/shard_map/ppermute | solution.py:68
  69.5 4.6 %collective-permute-start.10 = (bf16[48,4096]{1,0:T(8,128)(2,1)S(1)}, bf16[48,4096]{1,0:T(8,128)(2,1)S(1)}, u32[]{:S(2)}, u32[]{:S(2)}) collective-permute-start(bf16[48,4096]{1,0:T(8,128)(2,1)S(1)} %collective-permute-done.9), channel_id=1, source_target_pairs={{4,0},{8,4},{12,8},{16,12},{20,16},{24,20},{28,24},{32,28},{36,32}... | collective-permute-start | bytes 1179656 | tf_op jit(solution)/shard_map/ppermute | solution.py:70
  74.1 3.9 %collective-permute-done.3 = bf16[48,4096]{1,0:T(8,128)(2,1)S(1)} collective-permute-done((bf16[48,4096]{1,0:T(8,128)(2,1)S(1)}, bf16[48,4096]{1,0:T(8,128)(2,1)S(1)}, u32[]{:S(2)}, u32[]{:S(2)}) %collective-permute-start.3) | collective-permute-done | bytes 393248 | tf_op jit(solution)/shard_map/ppermute | solution.py:68
  80.0 4.6 %collective-permute-start.11 = (bf16[48,4096]{1,0:T(8,128)(2,1)S(1)}, bf16[48,4096]{1,0:T(8,128)(2,1)S(1)}, u32[]{:S(2)}, u32[]{:S(2)}) collective-permute-start(bf16[48,4096]{1,0:T(8,128)(2,1)S(1)} %collective-permute-done.10), channel_id=1, source_target_pairs={{4,0},{8,4},{12,8},{16,12},{20,16},{24,20},{28,24},{32,28},{36,32}... | collective-permute-start | bytes 1179656 | tf_op jit(solution)/shard_map/ppermute | solution.py:70
  84.6 3.2 %collective-permute-done.4 = bf16[48,4096]{1,0:T(8,128)(2,1)S(1)} collective-permute-done((bf16[48,4096]{1,0:T(8,128)(2,1)S(1)}, bf16[48,4096]{1,0:T(8,128)(2,1)S(1)}, u32[]{:S(2)}, u32[]{:S(2)}) %collective-permute-start.4) | collective-permute-done | bytes 393248 | tf_op jit(solution)/shard_map/ppermute | solution.py:68
  90.5 4.6 %collective-permute-start.12 = (bf16[48,4096]{1,0:T(8,128)(2,1)S(1)}, bf16[48,4096]{1,0:T(8,128)(2,1)}, u32[]{:S(2)}, u32[]{:S(2)}) collective-permute-start(bf16[48,4096]{1,0:T(8,128)(2,1)S(1)} %collective-permute-done.11), channel_id=1, source_target_pairs={{4,0},{8,4},{12,8},{16,12},{20,16},{24,20},{28,24},{32,28},{36,32}... | collective-permute-start | bytes 1179656 | tf_op jit(solution)/shard_map/ppermute | solution.py:70
  95.0 2.5 collective-permute-done.5
  99.8 5.1 %collective-permute-start.13 = (bf16[48,4096]{1,0:T(8,128)(2,1)}, bf16[48,4096]{1,0:T(8,128)(2,1)}, u32[]{:S(2)}, u32[]{:S(2)}) collective-permute-start(bf16[48,4096]{1,0:T(8,128)(2,1)} %collective-permute-done.12), channel_id=1, source_target_pairs={{4,0},{8,4},{12,8},{16,12},{20,16},{24,20},{28,24},{32,28},{36,32}... | collective-permute-start | bytes 1179656 | tf_op jit(solution)/shard_map/ppermute | solution.py:70
  104.9 2.7 %collective-permute-done.6 = bf16[48,4096]{1,0:T(8,128)(2,1)} collective-permute-done((bf16[48,4096]{1,0:T(8,128)(2,1)S(1)}, bf16[48,4096]{1,0:T(8,128)(2,1)}, u32[]{:S(2)}, u32[]{:S(2)}) %collective-permute-start.6) | collective-permute-done | bytes 393248 | tf_op jit(solution)/shard_map/ppermute | solution.py:68
  110.1 5.0 %collective-permute-start.14 = (bf16[48,4096]{1,0:T(8,128)(2,1)}, bf16[48,4096]{1,0:T(8,128)(2,1)S(1)}, u32[]{:S(2)}, u32[]{:S(2)}) collective-permute-start(bf16[48,4096]{1,0:T(8,128)(2,1)} %collective-permute-done.13), channel_id=1, source_target_pairs={{4,0},{8,4},{12,8},{16,12},{20,16},{24,20},{28,24},{32,28},{36,32}... | collective-permute-start | bytes 1179656 | tf_op jit(solution)/shard_map/ppermute | solution.py:70
  115.2 3.6 %collective-permute-done.7 = bf16[48,4096]{1,0:T(8,128)(2,1)} collective-permute-done((bf16[48,4096]{1,0:T(8,128)(2,1)}, bf16[48,4096]{1,0:T(8,128)(2,1)}, u32[]{:S(2)}, u32[]{:S(2)}) %collective-permute-start.7) | collective-permute-done | bytes 393248 | tf_op jit(solution)/shard_map/ppermute | solution.py:68
  139.3 6.4 %gather_fusion = bf16[16,48,4096]{2,1,0:T(8,128)(2,1)} fusion(bf16[16,48,4096]{2,1,0:T(8,128)(2,1)} %bitcast_dynamic-update-slice_fusion, s32[1024]{0:T(1024)S(1)} %pad_clamp_fusion.1), kind=kCustom, calls=%fused_computation | custom fusion | bytes 12582976 | tf_op jit(solution)/shard_map/gather | solution.py:73
  145.7 4.7 %fusion.4 = f32[768,128]{1,0:T(8,128)S(1)} fusion(bf16[768,4096]{1,0:T(8,128)(2,1)} %bitcast.64, bf16[1,4096,128]{2,1,0:T(8,128)(2,1)S(1)} %copy-done.13), kind=kOutput, calls=%fused_computation.8 | convolution fusion | flops 805306368 | bytes 7733248 | tf_op jit(solution)/shard_map/dot_general | solution.py:75
  152.6 12.2 %all_to_all.16 = bf16[4,768,128]{1,2,0:T(8,128)(2,1)S(1)} all-to-all(bf16[4,768,128]{1,2,0:T(8,128)(2,1)S(1)} %broadcast_in_dim.2), channel_id=1, replica_groups=mesh['expert'=8,'dp'=16,'tensor'=4] {'tensor'}, dimensions={0} | all-to-all | bytes 1572864 | tf_op jit(solution)/shard_map/all_to_all | solution.py:15
  164.8 2.7 fusion.1
  168.6 70.3 %reduce-scatter.2.cloned.1.call-done = f32[48,1024]{1,0:T(8,128)} async-done(((f32[768,1024]{1,0:T(8,128)}), f32[48,1024]{1,0:T(8,128)}) %reduce-scatter.2.cloned.1.call-update) | async-done | bytes 196624 | tf_op jit(solution)/shard_map/reduce_scatter | solution.py:79
  240.5 14.1 %all-to-all-start.2 = ((bf16[8,6,1024]{2,1,0:T(8,128)(2,1)}), bf16[8,6,1024]{2,1,0:T(8,128)(2,1)S(1)}, u32[]{:S(2)}, u32[]{:S(2)}) async-start(bf16[8,6,1024]{2,1,0:T(8,128)(2,1)} %reshape.126), calls=%async_computation.3 | async-start | bytes 262144 | tf_op jit(solution)/shard_map/all_to_all | solution.py:86
  254.6 5.2 %all-to-all-done.2 = bf16[8,6,1024]{2,1,0:T(8,128)(2,1)S(1)} async-done(((bf16[8,6,1024]{2,1,0:T(8,128)(2,1)}), bf16[8,6,1024]{2,1,0:T(8,128)(2,1)S(1)}, u32[]{:S(2)}, u32[]{:S(2)}) %all-to-all-start.2) | async-done | bytes 98336 | tf_op jit(solution)/shard_map/all_to_all | solution.py:86
  260.9 2.1 fusion.8
  (95 shorter events, 46.3 us)
Async XLA Ops:
  6.5 158.2 %copy-start = (bf16[1,512,1024]{2,1,0:T(8,128)(2,1)S(1)}, bf16[1,512,1024]{2,1,0:T(8,128)(2,1)}, u32[]{:S(2)}) copy-start(bf16[1,512,1024]{2,1,0:T(8,128)(2,1)} %param.13) | copy-start | bytes 3145732
  6.5 232.3 %reduce-scatter.2.cloned.1.call-start = ((), (), s32[]{:S(2)}) async-start(), calls=%async_computation.4 | async-start | bytes 3342336 | tf_op jit(solution)/shard_map/reduce_scatter | solution.py:79
  28.1 16.1 %collective-permute-start = (bf16[48,4096]{1,0:T(8,128)(2,1)S(1)}, bf16[48,4096]{1,0:T(8,128)(2,1)S(1)}, u32[]{:S(2)}, u32[]{:S(2)}) collective-permute-start(bf16[48,4096]{1,0:T(8,128)(2,1)S(1)} %reshape.123), channel_id=1, source_target_pairs={{0,4},{4,8},{8,12},{12,16},{16,20},{20,24},{24,28},{28,32},{32,36}... | collective-permute-start | bytes 1179656 | tf_op jit(solution)/shard_map/ppermute | solution.py:68
  44.2 12.1 %collective-permute-start.1 = (bf16[48,4096]{1,0:T(8,128)(2,1)S(1)}, bf16[48,4096]{1,0:T(8,128)(2,1)S(1)}, u32[]{:S(2)}, u32[]{:S(2)}) collective-permute-start(bf16[48,4096]{1,0:T(8,128)(2,1)S(1)} %collective-permute-done), channel_id=1, source_target_pairs={{0,4},{4,8},{8,12},{12,16},{16,20},{20,24},{24,28},{28,32},{32,36}... | collective-permute-start | bytes 1179656 | tf_op jit(solution)/shard_map/ppermute | solution.py:68
  46.1 12.2 %collective-permute-start.8 = (bf16[48,4096]{1,0:T(8,128)(2,1)S(1)}, bf16[48,4096]{1,0:T(8,128)(2,1)S(1)}, u32[]{:S(2)}, u32[]{:S(2)}) collective-permute-start(bf16[48,4096]{1,0:T(8,128)(2,1)S(1)} %reshape.123), channel_id=1, source_target_pairs={{4,0},{8,4},{12,8},{16,12},{20,16},{24,20},{28,24},{32,28},{36,32}... | collective-permute-start | bytes 1179656 | tf_op jit(solution)/shard_map/ppermute | solution.py:70
  56.3 11.3 %collective-permute-start.2 = (bf16[48,4096]{1,0:T(8,128)(2,1)S(1)}, bf16[48,4096]{1,0:T(8,128)(2,1)S(1)}, u32[]{:S(2)}, u32[]{:S(2)}) collective-permute-start(bf16[48,4096]{1,0:T(8,128)(2,1)S(1)} %collective-permute-done.1), channel_id=1, source_target_pairs={{0,4},{4,8},{8,12},{12,16},{16,20},{20,24},{24,28},{28,32},{32,36}... | collective-permute-start | bytes 1179656 | tf_op jit(solution)/shard_map/ppermute | solution.py:68
  58.3 11.3 %collective-permute-start.9 = (bf16[48,4096]{1,0:T(8,128)(2,1)S(1)}, bf16[48,4096]{1,0:T(8,128)(2,1)S(1)}, u32[]{:S(2)}, u32[]{:S(2)}) collective-permute-start(bf16[48,4096]{1,0:T(8,128)(2,1)S(1)} %collective-permute-done.8), channel_id=1, source_target_pairs={{4,0},{8,4},{12,8},{16,12},{20,16},{24,20},{28,24},{32,28},{36,32}... | collective-permute-start | bytes 1179656 | tf_op jit(solution)/shard_map/ppermute | solution.py:70
  67.6 10.4 %collective-permute-start.3 = (bf16[48,4096]{1,0:T(8,128)(2,1)S(1)}, bf16[48,4096]{1,0:T(8,128)(2,1)S(1)}, u32[]{:S(2)}, u32[]{:S(2)}) collective-permute-start(bf16[48,4096]{1,0:T(8,128)(2,1)S(1)} %collective-permute-done.2), channel_id=1, source_target_pairs={{0,4},{4,8},{8,12},{12,16},{16,20},{20,24},{24,28},{28,32},{32,36}... | collective-permute-start | bytes 1179656 | tf_op jit(solution)/shard_map/ppermute | solution.py:68
  69.5 10.4 %collective-permute-start.10 = (bf16[48,4096]{1,0:T(8,128)(2,1)S(1)}, bf16[48,4096]{1,0:T(8,128)(2,1)S(1)}, u32[]{:S(2)}, u32[]{:S(2)}) collective-permute-start(bf16[48,4096]{1,0:T(8,128)(2,1)S(1)} %collective-permute-done.9), channel_id=1, source_target_pairs={{4,0},{8,4},{12,8},{16,12},{20,16},{24,20},{28,24},{32,28},{36,32}... | collective-permute-start | bytes 1179656 | tf_op jit(solution)/shard_map/ppermute | solution.py:70
  78.1 21.7 %copy-start.7 = (bf16[48,4096]{1,0:T(8,128)(2,1)}, bf16[48,4096]{1,0:T(8,128)(2,1)S(1)}, u32[]{:S(2)}) copy-start(bf16[48,4096]{1,0:T(8,128)(2,1)S(1)} %collective-permute-done.3) | copy-start | bytes 1179652
  78.1 9.7 %collective-permute-start.4 = (bf16[48,4096]{1,0:T(8,128)(2,1)S(1)}, bf16[48,4096]{1,0:T(8,128)(2,1)S(1)}, u32[]{:S(2)}, u32[]{:S(2)}) collective-permute-start(bf16[48,4096]{1,0:T(8,128)(2,1)S(1)} %collective-permute-done.3), channel_id=1, source_target_pairs={{0,4},{4,8},{8,12},{12,16},{16,20},{20,24},{24,28},{28,32},{32,36}... | collective-permute-start | bytes 1179656 | tf_op jit(solution)/shard_map/ppermute | solution.py:68
  80.0 9.7 %collective-permute-start.11 = (bf16[48,4096]{1,0:T(8,128)(2,1)S(1)}, bf16[48,4096]{1,0:T(8,128)(2,1)S(1)}, u32[]{:S(2)}, u32[]{:S(2)}) collective-permute-start(bf16[48,4096]{1,0:T(8,128)(2,1)S(1)} %collective-permute-done.10), channel_id=1, source_target_pairs={{4,0},{8,4},{12,8},{16,12},{20,16},{24,20},{28,24},{32,28},{36,32}... | collective-permute-start | bytes 1179656 | tf_op jit(solution)/shard_map/ppermute | solution.py:70
  87.8 17.1 %copy-start.8 = (bf16[48,4096]{1,0:T(8,128)(2,1)}, bf16[48,4096]{1,0:T(8,128)(2,1)S(1)}, u32[]{:S(2)}) copy-start(bf16[48,4096]{1,0:T(8,128)(2,1)S(1)} %collective-permute-done.4) | copy-start | bytes 1179652
  87.8 9.7 %collective-permute-start.5 = (bf16[48,4096]{1,0:T(8,128)(2,1)S(1)}, bf16[48,4096]{1,0:T(8,128)(2,1)S(1)}, u32[]{:S(2)}, u32[]{:S(2)}) collective-permute-start(bf16[48,4096]{1,0:T(8,128)(2,1)S(1)} %collective-permute-done.4), channel_id=1, source_target_pairs={{0,4},{4,8},{8,12},{12,16},{16,20},{20,24},{24,28},{28,32},{32,36}... | collective-permute-start | bytes 1179656 | tf_op jit(solution)/shard_map/ppermute | solution.py:68
  90.5 9.3 %collective-permute-start.12 = (bf16[48,4096]{1,0:T(8,128)(2,1)S(1)}, bf16[48,4096]{1,0:T(8,128)(2,1)}, u32[]{:S(2)}, u32[]{:S(2)}) collective-permute-start(bf16[48,4096]{1,0:T(8,128)(2,1)S(1)} %collective-permute-done.11), channel_id=1, source_target_pairs={{4,0},{8,4},{12,8},{16,12},{20,16},{24,20},{28,24},{32,28},{36,32}... | collective-permute-start | bytes 1179656 | tf_op jit(solution)/shard_map/ppermute | solution.py:70
  97.5 10.1 %collective-permute-start.6 = (bf16[48,4096]{1,0:T(8,128)(2,1)S(1)}, bf16[48,4096]{1,0:T(8,128)(2,1)}, u32[]{:S(2)}, u32[]{:S(2)}) collective-permute-start(bf16[48,4096]{1,0:T(8,128)(2,1)S(1)} %collective-permute-done.5), channel_id=1, source_target_pairs={{0,4},{4,8},{8,12},{12,16},{16,20},{20,24},{24,28},{28,32},{32,36}... | collective-permute-start | bytes 1179656 | tf_op jit(solution)/shard_map/ppermute | solution.py:68
  99.8 10.4 %collective-permute-start.13 = (bf16[48,4096]{1,0:T(8,128)(2,1)}, bf16[48,4096]{1,0:T(8,128)(2,1)}, u32[]{:S(2)}, u32[]{:S(2)}) collective-permute-start(bf16[48,4096]{1,0:T(8,128)(2,1)} %collective-permute-done.12), channel_id=1, source_target_pairs={{4,0},{8,4},{12,8},{16,12},{20,16},{24,20},{28,24},{32,28},{36,32}... | collective-permute-start | bytes 1179656 | tf_op jit(solution)/shard_map/ppermute | solution.py:70
  107.6 11.1 %collective-permute-start.7 = (bf16[48,4096]{1,0:T(8,128)(2,1)}, bf16[48,4096]{1,0:T(8,128)(2,1)}, u32[]{:S(2)}, u32[]{:S(2)}) collective-permute-start(bf16[48,4096]{1,0:T(8,128)(2,1)} %collective-permute-done.6), channel_id=1, source_target_pairs={{0,4},{4,8},{8,12},{12,16},{16,20},{20,24},{24,28},{28,32},{32,36}... | collective-permute-start | bytes 1179656 | tf_op jit(solution)/shard_map/ppermute | solution.py:68
  109.7 23.6 %copy-start.4 = (bf16[48,4096]{1,0:T(8,128)(2,1)S(1)}, bf16[48,4096]{1,0:T(8,128)(2,1)}, u32[]{:S(2)}) copy-start(bf16[48,4096]{1,0:T(8,128)(2,1)} %copy-done.3) | copy-start | bytes 1179652
  109.7 24.4 %copy-start.6 = (bf16[48,4096]{1,0:T(8,128)(2,1)S(1)}, bf16[48,4096]{1,0:T(8,128)(2,1)}, u32[]{:S(2)}) copy-start(bf16[48,4096]{1,0:T(8,128)(2,1)} %copy-done.5) | copy-start | bytes 1179652
  110.1 28.3 %collective-permute-start.14 = (bf16[48,4096]{1,0:T(8,128)(2,1)}, bf16[48,4096]{1,0:T(8,128)(2,1)S(1)}, u32[]{:S(2)}, u32[]{:S(2)}) collective-permute-start(bf16[48,4096]{1,0:T(8,128)(2,1)} %collective-permute-done.13), channel_id=1, source_target_pairs={{4,0},{8,4},{12,8},{16,12},{20,16},{24,20},{28,24},{32,28},{36,32}... | collective-permute-start | bytes 1179656 | tf_op jit(solution)/shard_map/ppermute | solution.py:70
  152.4 15.3 %copy-start.12 = (f32[9]{0:T(128)S(1)}, f32[9]{0:T(128)}, u32[]{:S(2)}) copy-start(f32[9]{0:T(128)} %param.15) | copy-start | bytes 112
  152.4 15.9 %copy-start.10 = (bf16[8,16,1024]{2,1,0:T(8,128)(2,1)S(1)}, bf16[8,16,1024]{2,1,0:T(8,128)(2,1)}, u32[]{:S(2)}) copy-start(bf16[8,16,1024]{2,1,0:T(8,128)(2,1)} %param.14) | copy-start | bytes 786436
  240.5 19.3 %all-to-all-start.2 = ((bf16[8,6,1024]{2,1,0:T(8,128)(2,1)}), bf16[8,6,1024]{2,1,0:T(8,128)(2,1)S(1)}, u32[]{:S(2)}, u32[]{:S(2)}) async-start(bf16[8,6,1024]{2,1,0:T(8,128)(2,1)} %reshape.126), calls=%async_computation.3 | async-start | bytes 262144 | tf_op jit(solution)/shard_map/all_to_all | solution.py:86
  (8 other events, 59.0 us)
Sparse Core Ops, SparseCore 0:
  167.6 71.2 reduce-scatter.1
